TPU v7x, 32 devices: a whole 2x2x4 slice. The times are simulated.
32 devices in a mesh: band: 8 (over z, y), grid: 4 (over x, core).
Axes of the slice: x: 2, y: 2, z: 4, core: 2. Of those that a mesh axis runs over, the one named last changes fastest.
Arguments:
- orbitals: float32 [24, 64, 4096], P('band', 'grid'), may hold values from -6 to 6
- pair_mask: int32 [24, 24], replicated, may hold values from 0 to 1, as said below
Outputs:
- exchange_term: float32 [24, 64, 4096], P('band', 'grid')
Inputs may be any that keep to these rules, and one draw needn't show every extreme that they name: pair_mask is symmetric; entries outside the candidate pairs of every block (and their transposes) are 0; each block has at most 12 candidate pairs with mask 1, and some block has exactly 12.
All inputs are finite; a program needn't handle non-finite values.
Results may differ from a plain program's by a relative error of at most 0.00027.
Values sent between devices are 32-bit elements; how exact they have to be, the bound alone decides.
A program may use at most 64 MiB of HBM per device.

v0:
```python
import functools
import math

import jax
import jax.numpy as jnp
import numpy as np
from jax import lax
from jax.experimental import pallas as pl
from jax.experimental.pallas import tpu as pltpu
from jax.sharding import PartitionSpec as P

MESH = pl.DeviceIdType.MESH
MIXING = 0.25
BOX_LENGTH = 16.0
UNROLL = 16
SKEW = 4

PEER, CROSS, RELAY, DOWN, SIDE, SIDE_BACK, UP_BACK, REDUCE = 0, 3, 6, 9, 13, 17, 21, 25
COPIES = 34


def transform_tables(n):
    ids = np.arange(n)
    angles = (ids[:, None] * ids[None, :] % n) * (2.0 * np.pi / n)
    cas = np.cos(angles) + np.sin(angles)
    high = cas.astype(jnp.bfloat16).astype(np.float64)
    low = cas - high
    none = np.zeros_like(high)
    left = np.block([[high, high], [low, none]])
    both = lambda m: np.block([[m, none], [none, m]])
    right = np.block([[both(high), both(low)], [both(high), np.zeros((2 * n, 2 * n))]])
    return jnp.asarray(left, jnp.bfloat16), jnp.asarray(right, jnp.bfloat16)


def split(values, axis):
    high = values.astype(jnp.bfloat16)
    low = (values - high.astype(jnp.float32)).astype(jnp.bfloat16)
    return jnp.concatenate([high, low], axis=axis)


def left_product(left, values):
    both = jnp.dot(left, split(values, 0), preferred_element_type=jnp.float32)
    half = both.shape[0] // 2
    return both[:half] + both[half:]


def right_product(values, right):
    both = jnp.dot(split(values, 1), right, preferred_element_type=jnp.float32)
    half = both.shape[1] // 2
    return both[:, :half] + both[:, half:]


def fill_coulomb(n, coulomb):
    lanes = 2 * n
    scale = -MIXING * BOX_LENGTH * BOX_LENGTH / math.pi / float(n**3)

    def signed(index):
        return jnp.where(index < n // 2, index, index - n)

    def body(kx, carry):
        fx = signed(kx)
        fy = signed(lax.broadcasted_iota(jnp.int32, (n, lanes), 0))
        fz = signed(lax.broadcasted_iota(jnp.int32, (n, lanes), 1) % n)
        squared = fx * fx + fy * fy + fz * fz
        safe = jnp.maximum(squared, 1).astype(jnp.float32)
        coulomb[pl.ds(pl.multiple_of(kx * n, n), n), :] = jnp.where(squared > 0, scale / safe, 0.0)
        return carry

    lax.fori_loop(0, n, body, 0)


def potentials(n, phi, pot, coulomb, work, left_ref, right_ref, pairs):
    lanes, half, stride = 2 * n, n // 2, n + SKEW
    unroll = min(UNROLL, half)
    (ia, ta, wa, ca), (ib, tb, wb, cb) = pairs
    lower = lax.broadcasted_iota(jnp.int32, (n, lanes), 1) < n

    def cols(c):
        return pl.ds(pl.multiple_of(c * lanes, lanes), lanes)

    def forward(step, carry):
        left, right = left_ref[...], right_ref[...]
        rows = []
        for u in range(unroll):
            c = step * unroll + u
            first = phi[ia, :, cols(c)] * phi[ta, :, cols(c)] * wa
            second = phi[ib, :, cols(c)] * phi[tb, :, cols(c)] * wb
            turned = pltpu.roll(jnp.where(lower, second, first), n, 1)
            rows += [jnp.where(lower, first, turned), jnp.where(lower, turned, second)]
        along_z = right_product(jnp.concatenate(rows, axis=0), right)
        for u in range(unroll):
            c = step * unroll + u
            even, odd = along_z[2 * u * n:(2 * u + 1) * n], along_z[(2 * u + 1) * n:(2 * u + 2) * n]
            along_x = left_product(left, jnp.concatenate([even, odd], axis=1))
            work[pl.ds(2 * c * stride, n), :] = along_x[:, :lanes]
            work[pl.ds((2 * c + 1) * stride, n), :] = along_x[:, lanes:]
        return carry

    def middle(step, carry):
        left = left_ref[...]
        for u in range(unroll):
            kx = (step * unroll + u) * 2
            here = [pl.ds(kx + j, n, stride=stride) for j in range(2)]
            factor = [coulomb[pl.ds(pl.multiple_of((kx + j) * n, n), n), :] for j in range(2)]
            spectrum = left_product(left, jnp.concatenate([work[h, :] for h in here], axis=1))
            solved = left_product(left, spectrum * jnp.concatenate(factor, axis=1))
            work[here[0], :] = solved[:, :lanes]
            work[here[1], :] = solved[:, lanes:]
        return carry

    def inverse(step, carry):
        left, right = left_ref[...], right_ref[...]
        rows = []
        for u in range(unroll):
            c = step * unroll + u
            planes = [work[pl.ds((2 * c + j) * stride, n), :] for j in range(2)]
            along_x = left_product(left, jnp.concatenate(planes, axis=1))
            rows += [along_x[:, :lanes], along_x[:, lanes:]]
        along_z = right_product(jnp.concatenate(rows, axis=0), right)
        for u in range(unroll):
            c = step * unroll + u
            even, odd = along_z[2 * u * n:(2 * u + 1) * n], along_z[(2 * u + 1) * n:(2 * u + 2) * n]
            turned = pltpu.roll(jnp.where(lower, odd, even), n, 1)
            found = (jnp.where(lower, even, turned), jnp.where(lower, turned, odd))
            for value, (i, t, _, cross) in zip(found, pairs):
                pot[i, :, cols(c)] += value * phi[t, :, cols(c)]
                pot[t, :, cols(c)] += value * phi[i, :, cols(c)] * cross
        return carry

    lax.fori_loop(0, half // unroll, forward, 0)
    lax.fori_loop(0, half // unroll, middle, 0)
    lax.fori_loop(0, half // unroll, inverse, 0)


def kernel(groups, mask_ref, mine_ref, left_ref, right_ref, out_ref,
           phi, pot, coulomb, work, side, up, red, send_sem, recv_sem):
    orbs, planes, cells = mine_ref.shape
    n = phi.shape[1]
    band, grid = lax.axis_index("band"), lax.axis_index("grid")
    last = grid // orbs
    odd_band = lax.rem(band, 2)
    below, above = lax.rem(band + groups - 2, groups), lax.rem(band + 2, groups)
    beside = band + 1 - 2 * odd_band
    peer, across, far = grid + 1 - 2 * lax.rem(grid, 2), lax.rem(grid + 2, 4), 3 - grid
    other = {1: peer, 2: across, 3: far}
    shares = grid < orbs
    even_shares = shares & (odd_band == 0)
    odd_shares = shares & (odd_band == 1)

    def order(device):
        first = device - device // orbs
        second = 1 - (device + 2) // orbs
        return first, second, orbs - first - second

    def rows(quarter):
        return pl.ds(pl.multiple_of(quarter * planes, planes), planes)

    def copy(source, target, number, device):
        return pltpu.make_async_remote_copy(
            src_ref=source, dst_ref=target, send_sem=send_sem.at[number], recv_sem=recv_sem.at[number],
            device_id=device, device_id_type=MESH)

    def arrived(target, number):
        copy(target, target, number, (band, peer)).wait_recv()

    def left_here(target, number):
        copy(target, target, number, (band, peer)).wait_send()

    barrier = pltpu.get_barrier_semaphore()
    for device in ((band, peer), (band, across), (band, far), (beside, grid), (below, grid), (above, grid)):
        pl.semaphore_signal(barrier, inc=1, device_id=device, device_id_type=MESH)
    pl.semaphore_wait(barrier, 6)

    quarters = (grid, peer, across, far)

    def pass_on(k, source):
        @pl.when(shares)
        def _():
            copy(source, phi.at[4, rows(quarters[k])], DOWN + k, (below, grid)).start()

        @pl.when(odd_shares)
        def _():
            copy(source, phi.at[3, rows(quarters[k])], SIDE + k, (beside, grid)).start()

    def side_relay(k):
        @pl.when(even_shares)
        def _():
            arrived(phi.at[4, rows(quarters[k])], DOWN + k)
            copy(phi.at[4, rows(quarters[k])], phi.at[3, rows(quarters[k])], SIDE + k, (beside, grid)).start()

    pass_on(0, mine_ref.at[lax.rem(grid, orbs)])
    for k, i in enumerate(order(across)):
        copy(mine_ref.at[i], phi.at[i, rows(grid)], CROSS + k, (band, across)).start()
    for k, i in enumerate(order(peer)):
        copy(mine_ref.at[i], phi.at[i, rows(grid)], PEER + k, (band, peer)).start()
    for i in range(orbs):
        phi[i, rows(grid), :] = mine_ref[i]

    mine, theirs = order(grid), order(peer)
    arrived(phi.at[mine[0], rows(peer)], PEER)
    pass_on(1, phi.at[mine[0], rows(peer)])
    fill_coulomb(n, coulomb)
    pot[...] = jnp.zeros_like(pot)

    def relay(k):
        arrived(phi.at[mine[k], rows(across)], CROSS + k)
        copy(phi.at[mine[k], rows(across)], phi.at[mine[k], rows(across)], RELAY + k, (band, peer)).start()

    side_relay(0)
    relay(0)
    pass_on(2, phi.at[mine[0], rows(across)])
    side_relay(1)
    relay(1)
    wanted = 1 - grid // 2

    @pl.when(shares)
    def _():
        arrived(phi.at[grid, rows(far)], RELAY + wanted)

    pass_on(3, phi.at[mine[0], rows(far)])
    side_relay(2)
    relay(2)
    side_relay(3)

    for k in range(1, orbs):
        arrived(phi.at[mine[k], rows(peer)], PEER + k)
    for k in range(orbs):
        @pl.when((last == 1) | (k != wanted))
        def _():
            arrived(phi.at[theirs[k], rows(far)], RELAY + k)

    @pl.when(odd_shares)
    def _():
        for k in range(4):
            arrived(phi.at[4, rows(quarters[k])], DOWN + k)

    def step(index, carry):
        @pl.when(shares & (index == 1))
        def _():
            for k in range(4):
                arrived(phi.at[3, rows(quarters[k])], SIDE + k)

        pairs = []
        for lane_half in range(2):
            number = 2 * index + lane_half
            near = number // orbs
            i = lax.rem(number, orbs)
            within = lax.rem(i + 1 - near, orbs)
            t = last * within + (1 - last) * (4 - near)
            ahead = lax.rem(band + 2 - near, groups)
            column = last * (band * orbs + within) + (1 - last) * (ahead * orbs + grid)
            weight = mask_ref[band * orbs + i, column].astype(jnp.float32)
            pairs.append((i, t, weight, (1 - last * near).astype(jnp.float32)))
        potentials(n, phi, pot, coulomb, work, left_ref, right_ref, pairs)
        return carry

    lax.fori_loop(0, orbs, step, 0)

    back = (across, far, peer, grid)
    distance = (2, 3, 1)

    @pl.when(shares)
    def _():
        for k in range(4):
            copy(pot.at[3, rows(back[k])], side.at[rows(back[k])], SIDE_BACK + k, (beside, grid)).start()

    def up_send(k):
        copy(pot.at[4, rows(back[k])], up.at[rows(back[k])], UP_BACK + k, (above, grid)).start()

    @pl.when(odd_shares)
    def _():
        for k in range(4):
            up_send(k)

    def give(i, k):
        d = distance[k]
        copy(pot.at[i, rows(back[k])], red.at[d - 1, i], REDUCE + (d - 1) * orbs + i, (band, other[d])).start()

    for k in range(3):
        for shift in (1, 2):
            give(lax.rem(grid + shift, orbs), k)

    @pl.when(last == 1)
    def _():
        for k in range(3):
            give(0, k)

    def join(k):
        @pl.when(even_shares)
        def _():
            arrived(side.at[rows(back[k])], SIDE_BACK + k)
            pot[4, rows(back[k]), :] += side[rows(back[k]), :]
            up_send(k)

    def collect(k):
        @pl.when(shares)
        def _():
            arrived(up.at[rows(back[k])], UP_BACK + k)
            pot[grid, rows(back[k]), :] += up[rows(back[k]), :]

        @pl.when(odd_shares)
        def _():
            arrived(side.at[rows(back[k])], SIDE_BACK + k)
            pot[grid, rows(back[k]), :] += side[rows(back[k]), :]

        if k < 3:
            @pl.when(shares)
            def _():
                give(grid, k)

    join(0)
    join(1)
    join(2)
    collect(0)
    join(3)
    for k in range(1, 4):
        collect(k)

    for i in range(orbs):
        for d in range(1, 4):
            arrived(red.at[d - 1, i], REDUCE + (d - 1) * orbs + i)
        out_ref[i] = (pot[i, rows(grid), :] + red[0, i]) + (red[1, i] + red[2, i])

    for number in (*range(PEER, DOWN), *range(REDUCE, COPIES)):
        left_here(out_ref.at[0], number)

    @pl.when(shares)
    def _():
        for number in range(DOWN, REDUCE):
            left_here(out_ref.at[0], number)


def local(groups, orbitals, pair_mask):
    orbs, planes, cells = orbitals.shape
    n = math.isqrt(cells)
    left, right = transform_tables(n)
    in_vmem = pl.BlockSpec(memory_space=pltpu.VMEM)
    cube = (n, cells)
    return pl.pallas_call(
        functools.partial(kernel, groups),
        out_shape=jax.ShapeDtypeStruct(orbitals.shape, jnp.float32),
        in_specs=[pl.BlockSpec(memory_space=pltpu.SMEM), in_vmem, in_vmem, in_vmem],
        out_specs=in_vmem,
        scratch_shapes=[
            pltpu.VMEM((orbs + 2, *cube), jnp.float32),
            pltpu.VMEM((orbs + 2, *cube), jnp.float32),
            pltpu.VMEM((n * n, 2 * n), jnp.float32),
            pltpu.VMEM((n * (n + SKEW), 2 * n), jnp.float32),
            pltpu.VMEM(cube, jnp.float32),
            pltpu.VMEM(cube, jnp.float32),
            pltpu.VMEM((3, orbs, planes, cells), jnp.float32),
            pltpu.SemaphoreType.DMA((COPIES,)),
            pltpu.SemaphoreType.DMA((COPIES,)),
        ],
        compiler_params=pltpu.CompilerParams(
            collective_id=0, has_side_effects=True, vmem_limit_bytes=48 * 2**20),
    )(pair_mask, orbitals, left, right)


def solution(mesh):
    groups, parts = mesh.shape["band"], mesh.shape["grid"]
    assert parts == 4 and groups % 2 == 0 and groups >= 4
    return jax.shard_map(
        functools.partial(local, groups),
        mesh=mesh,
        in_specs=(P("band", "grid", None), P()),
        out_specs=P("band", "grid", None),
        check_vma=False,
    )
```

profile of v0, /device:TPU:0, one launch (start us, length us, event | category | flops | bytes accessed | tf_op | source)
XLA Modules:
  0.0 86.3 jit_solution(16476373439791172240)
XLA Ops:
  0.0 0.0 copy-start
  0.0 1.1 %copy-done = f32[3,16,4096]{2,1,0:T(8,128)S(1)} copy-done((f32[3,16,4096]{2,1,0:T(8,128)S(1)}, f32[3,16,4096]{2,1,0:T(8,128)}, u32[]{:S(2)}) %copy-start) | copy-done | bytes 786456
  1.1 0.0 copy-start.1
  1.1 0.9 %copy-done.1 = bf16[256,256]{1,0:T(8,128)(2,1)S(1)} copy-done((bf16[256,256]{1,0:T(8,128)(2,1)S(1)}, bf16[256,256]{1,0:T(8,128)(2,1)}, u32[]{:S(2)}) %copy-start.1) | copy-done | bytes 131096
  2.0 0.0 copy-start.2
  2.0 0.8 copy-done.2
  2.8 0.0 copy-start.3
  2.8 0.7 copy-done.3
  3.5 81.9 %shard_map.46 = f32[3,16,4096]{2,1,0:T(8,128)S(1)} custom-call(s32[24,24]{1,0:T(8,128)S(1)} %copy-done.3, f32[3,16,4096]{2,1,0:T(8,128)S(1)} %copy-done, bf16[128,128]{1,0:T(8,128)(2,1)S(1)} %copy-done.2, bf16[256,256]{1,0:T(8,128)(2,1)S(1)} %copy-done.1), custom_call_target="tpu_custom_call" | custom-call | tf_op jit(solution)/shard_map/pallas_call | solution.py:339
  85.4 0.9 %copy.6 = f32[3,16,4096]{2,1,0:T(8,128)} copy(f32[3,16,4096]{2,1,0:T(8,128)S(1)} %shard_map.46) | data formatting | bytes 1572864
Async XLA Ops:
  0.0 1.1 %copy-start = (f32[3,16,4096]{2,1,0:T(8,128)S(1)}, f32[3,16,4096]{2,1,0:T(8,128)}, u32[]{:S(2)}) copy-start(f32[3,16,4096]{2,1,0:T(8,128)} %mine_ref.1) | copy-start | bytes 2359300
  1.1 0.9 %copy-start.1 = (bf16[256,256]{1,0:T(8,128)(2,1)S(1)}, bf16[256,256]{1,0:T(8,128)(2,1)}, u32[]{:S(2)}) copy-start(bf16[256,256]{1,0:T(8,128)(2,1)} %constant.5.clone.right_ref) | copy-start | bytes 393220
  2.0 0.8 copy-start.2
  2.8 0.7 copy-start.3
where the time goes:
time: 86.6 us; the launch traced here: 86.3 us
  Pallas kernels  81.9 us (95%)
  local copies, waits for them, and re-layouts  4.38 us (5%)
    pallas_call x1, Pallas kernels, local(): pl.pallas_call(functools.partial(kernel, groups), out_shape=jax.ShapeDtyp...  81.9 us
    unnamed x9, local copies, waits for them, and re-layouts  4.38 us

commit v1 on v0

v1 whole, which is shorter than its diff:
```python
import functools
import math

import jax
import jax.numpy as jnp
import numpy as np
from jax import lax
from jax.experimental import pallas as pl
from jax.experimental.pallas import tpu as pltpu
from jax.sharding import PartitionSpec as P

MESH = pl.DeviceIdType.MESH
MIXING = 0.25
BOX_LENGTH = 16.0
SKEW = 4

CHUNKS = 2

PEER = 0
CROSS = PEER + 3
RELAY = CROSS + 3 * CHUNKS
DOWN = RELAY + 3 * CHUNKS
SIDE = DOWN + 4 * CHUNKS
SIDE_BACK = SIDE + 4 * CHUNKS
UP_BACK = SIDE_BACK + 4 * CHUNKS
JOINT = UP_BACK + 4 * CHUNKS
COMB = JOINT + 3
FROM_PEER = COMB + 2
FROM_CHIP = FROM_PEER + 3 * CHUNKS
FAR = FROM_CHIP + 3 * CHUNKS
COPIES = FAR + CHUNKS


def transform_tables(n):
    ids = np.arange(n)
    angles = (ids[:, None] * ids[None, :] % n) * (2.0 * np.pi / n)
    cas = np.cos(angles) + np.sin(angles)
    high = cas.astype(jnp.bfloat16).astype(np.float64)
    low = cas - high
    none = np.zeros_like(high)
    left = np.block([[high, high], [low, none]])
    both = lambda m: np.block([[m, none], [none, m]])
    right = np.block([[both(high), both(low)], [both(high), np.zeros((2 * n, 2 * n))]])
    return jnp.asarray(left, jnp.bfloat16), jnp.asarray(right, jnp.bfloat16)


def split(values, axis):
    high = values.astype(jnp.bfloat16)
    low = (values - high.astype(jnp.float32)).astype(jnp.bfloat16)
    return jnp.concatenate([high, low], axis=axis)


def left_product(left, values):
    both = jnp.dot(left, split(values, 0), preferred_element_type=jnp.float32)
    half = both.shape[0] // 2
    return both[:half] + both[half:]


def right_product(values, right):
    both = jnp.dot(split(values, 1), right, preferred_element_type=jnp.float32)
    half = both.shape[1] // 2
    return both[:, :half] + both[:, half:]


def fill_coulomb(n, coulomb):
    lanes = 2 * n
    scale = -MIXING * BOX_LENGTH * BOX_LENGTH / math.pi / float(n**3)
    group = 4

    def signed(index):
        return jnp.where(index < n // 2, index, index - n)

    def body(step, carry):
        fy = signed(lax.broadcasted_iota(jnp.int32, (n, lanes), 0))
        fz = signed(lax.broadcasted_iota(jnp.int32, (n, lanes), 1) % n)
        plane = fy * fy + fz * fz
        for u in range(group):
            kx = step * group + u
            fx = signed(kx)
            squared = fx * fx + plane
            safe = jnp.maximum(squared, 1).astype(jnp.float32)
            coulomb[pl.ds(pl.multiple_of(kx * n, n), n), :] = jnp.where(squared > 0, scale / safe, 0.0)
        return carry

    lax.fori_loop(0, n // group, body, 0)


def densities(n, planes, phi, work, right_ref, quarter, pairs):
    lanes, half, stride = 2 * n, n // 2, n + SKEW
    (ia, ta, wa), (ib, tb, wb) = pairs
    start = quarter * planes
    rows = pl.ds(pl.multiple_of(start, planes), planes)
    lower = lax.broadcasted_iota(jnp.int32, (planes, lanes), 1) < n
    right = right_ref[...]
    block = half // 2
    for first_col in range(0, half, block):
        strips = []
        for c in range(first_col, first_col + block):
            cols = slice(c * lanes, (c + 1) * lanes)
            first = phi[ia, rows, cols] * phi[ta, rows, cols] * wa
            second = phi[ib, rows, cols] * phi[tb, rows, cols] * wb
            turned = pltpu.roll(jnp.where(lower, second, first), n, 1)
            strips += [jnp.where(lower, first, turned), jnp.where(lower, turned, second)]
        along_z = right_product(jnp.concatenate(strips, axis=0), right)
        for u in range(2 * block):
            y = 2 * first_col + u
            work[pl.ds(y * stride + start, planes), :] = along_z[u * planes:(u + 1) * planes]


def along_y(n, planes, work, left_ref, quarter):
    stride = n + SKEW
    left = left_ref[...]
    for u in range(planes // 2):
        here = [pl.ds(quarter * planes + 2 * u + j, n, stride=stride) for j in range(2)]
        done = left_product(left, jnp.concatenate([work[h, :] for h in here], axis=1))
        work[here[0], :] = done[:, :2 * n]
        work[here[1], :] = done[:, 2 * n:]


def along_x(n, work, coulomb, left_ref):
    stride = n + SKEW
    left = left_ref[...]
    for u in range(n // 2):
        here = [pl.ds((2 * u + j) * stride, n) for j in range(2)]
        factor = [coulomb[(2 * u + j) * n:(2 * u + j + 1) * n, :] for j in range(2)]
        spectrum = left_product(left, jnp.concatenate([work[h, :] for h in here], axis=1))
        done = left_product(left, spectrum * jnp.concatenate(factor, axis=1))
        work[here[0], :] = done[:, :2 * n]
        work[here[1], :] = done[:, 2 * n:]


def exchange_terms(n, planes, phi, pot, work, right_ref, quarter, last, partners):
    lanes, half, stride = 2 * n, n // 2, n + SKEW
    start = quarter * planes
    rows = pl.ds(pl.multiple_of(start, planes), planes)
    lower = lax.broadcasted_iota(jnp.int32, (planes, lanes), 1) < n
    right = right_ref[...]
    within = last.astype(jnp.float32)
    block = half // 4
    for first_col in range(0, half, block):
        solved = []
        for p in range(3):
            strips = [work[p, pl.ds(y * stride + start, planes), :]
                      for y in range(2 * first_col, 2 * (first_col + block))]
            solved.append(right_product(jnp.concatenate(strips, axis=0), right))
        for u in range(block):
            cols = slice((first_col + u) * lanes, (first_col + u + 1) * lanes)
            values = []
            for along_z in solved:
                even = along_z[2 * u * planes:(2 * u + 1) * planes]
                odd = along_z[(2 * u + 1) * planes:(2 * u + 2) * planes]
                turned = pltpu.roll(jnp.where(lower, odd, even), n, 1)
                values += [jnp.where(lower, even, turned), jnp.where(lower, turned, odd)]
            away, near = values[:3], values[3:]
            own = [phi[i, rows, cols] for i in range(3)]
            for i in range(3):
                before = (i + 2) % 3
                pot[i, rows, cols] = (away[i] * phi[partners[0][i], rows, cols]
                                      + near[i] * phi[partners[1][i], rows, cols]
                                      + away[before] * own[before] * within)
            pot[3, rows, cols] = near[0] * own[0] + near[1] * own[1] + near[2] * own[2]
            pot[4, rows, cols] = away[0] * own[0] + away[1] * own[1] + away[2] * own[2]


def kernel(groups, mask_hbm, mine_ref, left_hbm, right_hbm, out_ref,
           phi, pot, coulomb, work, side, up, comb, joint, from_peer, from_chip,
           left_ref, right_ref, mask_ref, load_sem, send_sem, recv_sem):
    orbs, planes, cells = mine_ref.shape
    n = phi.shape[1]
    depth = planes // CHUNKS
    band, grid = lax.axis_index("band"), lax.axis_index("grid")
    last = grid // orbs
    odd_band = lax.rem(band, 2)
    below, above = lax.rem(band + groups - 2, groups), lax.rem(band + 2, groups)
    beside = band + 1 - 2 * odd_band
    peer, across, far = grid + 1 - 2 * lax.rem(grid, 2), lax.rem(grid + 2, 4), 3 - grid
    shares, peer_shares = grid < orbs, peer < orbs
    even_shares = shares & (odd_band == 0)
    odd_shares = shares & (odd_band == 1)

    def order(device):
        first = device - device // orbs
        second = 1 - (device + 2) // orbs
        return first, second, orbs - first - second

    def rows(quarter):
        return pl.ds(pl.multiple_of(quarter * planes, planes), planes)

    def part(quarter, c):
        return pl.ds(pl.multiple_of(quarter * planes + c * depth, depth), depth)

    def copy(source, target, number, device, sent=None):
        return pltpu.make_async_remote_copy(
            src_ref=source, dst_ref=target, send_sem=send_sem.at[number if sent is None else sent],
            recv_sem=recv_sem.at[number], device_id=device, device_id_type=MESH)

    def arrived(target, number):
        copy(target, target, number, (band, peer)).wait_recv()

    def gone(target, number):
        copy(target, target, number, (band, peer)).wait_send()

    loads = [pltpu.make_async_copy(mine_ref.at[i], phi.at[i, rows(grid)], load_sem.at[i]) for i in range(orbs)]
    loads += [pltpu.make_async_copy(a, b, load_sem.at[orbs + k]) for k, (a, b) in enumerate(
        ((mask_hbm, mask_ref), (left_hbm, left_ref), (right_hbm, right_ref)))]
    for load in loads:
        load.start()

    barrier = pltpu.get_barrier_semaphore()
    for device in ((band, peer), (band, across), (band, far), (beside, grid), (below, grid), (above, grid)):
        pl.semaphore_signal(barrier, inc=1, device_id=device, device_id_type=MESH)
    for load in loads[:orbs]:
        load.wait()
    pl.semaphore_wait(barrier, 6)

    quarters = (grid, peer, across, far)

    def pass_on(k, c):
        piece = phi.at[lax.rem(grid, orbs), part(quarters[k], c)]

        @pl.when(shares)
        def _():
            copy(piece, phi.at[4, part(quarters[k], c)], DOWN + k * CHUNKS + c, (below, grid)).start()

        @pl.when(odd_shares)
        def _():
            copy(piece, phi.at[3, part(quarters[k], c)], SIDE + k * CHUNKS + c, (beside, grid)).start()

    def side_relay(m):
        k, c = divmod(m, CHUNKS)
        piece = phi.at[4, part(quarters[k], c)]

        @pl.when(even_shares)
        def _():
            arrived(piece, DOWN + m)
            copy(piece, phi.at[3, part(quarters[k], c)], SIDE + m, (beside, grid)).start()

    for c in range(CHUNKS):
        pass_on(0, c)
    for k, i in enumerate(order(across)):
        for c in range(CHUNKS):
            piece = phi.at[i, part(grid, c)]
            copy(piece, piece, CROSS + k * CHUNKS + c, (band, across)).start()
    for k, i in enumerate(order(peer)):
        piece = phi.at[i, rows(grid)]
        copy(piece, piece, PEER + k, (band, peer)).start()

    mine, theirs = order(grid), order(peer)
    arrived(phi.at[mine[0], rows(peer)], PEER)
    for c in range(CHUNKS):
        pass_on(1, c)
    fill_coulomb(n, coulomb)
    for load in loads[orbs:]:
        load.wait()

    def relay(k, c):
        piece = phi.at[mine[k], part(across, c)]
        arrived(piece, CROSS + k * CHUNKS + c)
        copy(piece, piece, RELAY + k * CHUNKS + c, (band, peer)).start()

    wanted = 1 - grid // 2

    def far_on(c):
        @pl.when(shares)
        def _():
            arrived(phi.at[grid, part(far, c)], RELAY + wanted * CHUNKS + c)

        pass_on(3, c)

    def partner(i, near):
        within = lax.rem(i + 1 - near, orbs)
        return last * within + (1 - last) * (4 - near)

    def forward(p, quarter):
        pairs = []
        for lane_half in range(2):
            number = 2 * p + lane_half
            near, i = number // orbs, lax.rem(number, orbs)
            ahead = lax.rem(band + 2 - near, groups)
            column = last * (band * orbs + lax.rem(i + 1 - near, orbs)) + (1 - last) * (ahead * orbs + grid)
            weight = mask_ref[band * orbs + i, column].astype(jnp.float32)
            pairs.append((i, partner(i, near), weight))
        densities(n, planes, phi, work.at[p], right_ref, quarter, pairs)
        along_y(n, planes, work.at[p], left_ref, quarter)

    def forward_rest(quarter):
        def body(p, carry):
            forward(p, quarter)
            return carry

        lax.fori_loop(1, 3, body, 0)

    def await_down(k):
        @pl.when(odd_shares)
        def _():
            for c in range(CHUNKS):
                arrived(phi.at[4, part(quarters[k], c)], DOWN + k * CHUNKS + c)

    def await_side(k):
        @pl.when(shares)
        def _():
            for c in range(CHUNKS):
                arrived(phi.at[3, part(quarters[k], c)], SIDE + k * CHUNKS + c)

    zero = lax.rem(grid, 1)
    for c in range(CHUNKS):
        relay(0, c)
        pass_on(2, c)
        side_relay(c)
    await_down(0)
    forward(zero, quarters[0])
    for c in range(CHUNKS):
        relay(1, c)
        side_relay(CHUNKS + c)
        far_on(c)
    await_down(1)
    for k in range(1, orbs):
        arrived(phi.at[mine[k], rows(peer)], PEER + k)
    forward(zero, quarters[1])
    for c in range(CHUNKS):
        side_relay(2 * CHUNKS + c)
        relay(2, c)
    await_down(2)
    forward(zero, quarters[2])
    for c in range(CHUNKS - 1):
        side_relay(3 * CHUNKS + c)
    for k in range(2):
        await_side(k)
        forward_rest(quarters[k])
    side_relay(4 * CHUNKS - 1)
    for k in range(orbs):
        @pl.when((last == 1) | (k != wanted))
        def _():
            for c in range(CHUNKS):
                arrived(phi.at[theirs[k], part(far, c)], RELAY + k * CHUNKS + c)
    await_down(3)
    forward(zero, quarters[3])

    def solve(p, carry):
        @pl.when(p == 1)
        def _():
            for k in (2, 3):
                await_side(k)
                forward_rest(quarters[k])

        along_x(n, work.at[p], coulomb, left_ref)
        return carry

    lax.fori_loop(0, 3, solve, 0)

    back = (across, far, peer, grid)
    partners = [[partner(i, near) for i in range(3)] for near in range(2)]

    def up_send(m):
        k, c = divmod(m, CHUNKS)
        copy(pot.at[4, part(back[k], c)], up.at[part(back[k], c)], UP_BACK + m, (above, grid)).start()

    def elsewhere(i):
        return grid // 2 != i // 2

    for k in range(4):
        def inverse(p, carry):
            along_y(n, planes, work.at[p], left_ref, back[k])
            return carry

        lax.fori_loop(0, 3, inverse, 0)
        exchange_terms(n, planes, phi, pot, work, right_ref, back[k], last, partners)

        @pl.when(shares)
        def _():
            for c in range(CHUNKS):
                here = part(back[k], c)
                copy(pot.at[3, here], side.at[here], SIDE_BACK + k * CHUNKS + c, (beside, grid)).start()

        @pl.when(odd_shares)
        def _():
            for c in range(CHUNKS):
                up_send(k * CHUNKS + c)

        if k == 1:
            for i in range(orbs):
                @pl.when(elsewhere(i))
                def _():
                    copy(pot.at[i, rows(far)], joint.at[i], JOINT + i, (band, peer)).start()

        if k < 2:
            @pl.when(peer_shares)
            def _():
                copy(pot.at[peer, rows(back[k])], comb.at[1 - k], COMB + 1 - k, (band, peer)).start()

        if k == 2:
            for i in range(orbs):
                @pl.when(elsewhere(i) | (peer == i))
                def _():
                    for c in range(CHUNKS):
                        copy(pot.at[i, part(peer, c)], from_peer.at[i, pl.ds(c * depth, depth)],
                             FROM_PEER + i * CHUNKS + c, (band, peer)).start()

    for i in range(orbs):
        @pl.when(elsewhere(i))
        def _():
            arrived(joint.at[i], JOINT + i)
            pot[i, rows(across), :] += joint[i]
            for c in range(CHUNKS):
                copy(pot.at[i, part(across, c)], from_chip.at[i, pl.ds(c * depth, depth)],
                     FROM_CHIP + i * CHUNKS + c, (band, across)).start()

    def join(m):
        k, c = divmod(m, CHUNKS)

        @pl.when(even_shares)
        def _():
            arrived(side.at[part(back[k], c)], SIDE_BACK + m)
            pot[4, part(back[k], c), :] += side[part(back[k], c), :]
            up_send(m)

    def collect(m):
        k, c = divmod(m, CHUNKS)
        here = part(back[k], c)
        inner = pl.ds(c * depth, depth)

        @pl.when(shares)
        def _():
            if k < 2 and c == 0:
                arrived(comb.at[k], COMB + k)
            arrived(up.at[here], UP_BACK + m)
            if k < 2:
                pot[grid, here, :] += up[here, :] + comb[k, inner, :]
            else:
                pot[grid, here, :] += up[here, :]

        @pl.when(odd_shares)
        def _():
            arrived(side.at[here], SIDE_BACK + m)
            pot[grid, here, :] += side[here, :]

        @pl.when(shares)
        def _():
            source = pot.at[grid, here]
            number = grid * CHUNKS + c
            if k == 0:
                copy(source, from_chip.at[grid, inner], FROM_CHIP + number, (band, across)).start()
            elif k == 1:
                copy(source, from_chip.at[grid, inner], FROM_CHIP + number, (band, far), FAR + c).start()
            elif k == 2:
                copy(source, from_peer.at[grid, inner], FROM_PEER + number, (band, peer)).start()

    join(0)
    join(1)
    for m in range(4 * CHUNKS):
        collect(m)
        if m + 2 < 4 * CHUNKS:
            join(m + 2)

    for i in range(orbs):
        for c in range(CHUNKS):
            inner = pl.ds(c * depth, depth)
            arrived(from_peer.at[i, inner], FROM_PEER + i * CHUNKS + c)
            arrived(from_chip.at[i, inner], FROM_CHIP + i * CHUNKS + c)
        out_ref[i] = pot[i, rows(grid), :] + from_peer[i] + from_chip[i]

    whole, chunk = comb.at[0], comb.at[0, pl.ds(0, depth)]
    for number in range(PEER, PEER + 3):
        gone(whole, number)
    for number in range(CROSS, DOWN):
        gone(chunk, number)

    @pl.when(shares)
    def _():
        for number in (*range(DOWN, JOINT), *range(FAR, FAR + CHUNKS)):
            gone(chunk, number)
        for c in range(CHUNKS):
            gone(chunk, FROM_CHIP + grid * CHUNKS + c)
            gone(chunk, FROM_PEER + grid * CHUNKS + c)

    @pl.when(peer_shares)
    def _():
        gone(whole, COMB)
        gone(whole, COMB + 1)
        for c in range(CHUNKS):
            gone(chunk, FROM_PEER + peer * CHUNKS + c)

    for i in range(orbs):
        @pl.when(elsewhere(i))
        def _():
            gone(whole, JOINT + i)
            for c in range(CHUNKS):
                gone(chunk, FROM_PEER + i * CHUNKS + c)
                gone(chunk, FROM_CHIP + i * CHUNKS + c)


def local(groups, orbitals, pair_mask):
    orbs, planes, cells = orbitals.shape
    n = math.isqrt(cells)
    left, right = transform_tables(n)
    in_hbm = pl.BlockSpec(memory_space=pltpu.HBM)
    cube, piece = (n, cells), (planes, cells)
    return pl.pallas_call(
        functools.partial(kernel, groups),
        out_shape=jax.ShapeDtypeStruct(orbitals.shape, jnp.float32),
        in_specs=[in_hbm] * 4,
        out_specs=pl.BlockSpec(memory_space=pltpu.VMEM),
        scratch_shapes=[
            pltpu.VMEM((orbs + 2, *cube), jnp.float32),
            pltpu.VMEM((orbs + 2, *cube), jnp.float32),
            pltpu.VMEM((n * n, 2 * n), jnp.float32),
            pltpu.VMEM((3, n * (n + SKEW), 2 * n), jnp.float32),
            pltpu.VMEM(cube, jnp.float32),
            pltpu.VMEM(cube, jnp.float32),
            pltpu.VMEM((2, *piece), jnp.float32),
            pltpu.VMEM((orbs, *piece), jnp.float32),
            pltpu.VMEM((orbs, *piece), jnp.float32),
            pltpu.VMEM((orbs, *piece), jnp.float32),
            pltpu.VMEM(left.shape, jnp.bfloat16),
            pltpu.VMEM(right.shape, jnp.bfloat16),
            pltpu.SMEM(pair_mask.shape, jnp.int32),
            pltpu.SemaphoreType.DMA((orbs + 3,)),
            pltpu.SemaphoreType.DMA((COPIES,)),
            pltpu.SemaphoreType.DMA((COPIES,)),
        ],
        compiler_params=pltpu.CompilerParams(
            collective_id=0, has_side_effects=True),
    )(pair_mask, orbitals, left, right)


def solution(mesh):
    groups, parts = mesh.shape["band"], mesh.shape["grid"]
    assert parts == 4 and groups % 2 == 0 and groups >= 4
    return jax.shard_map(
        functools.partial(local, groups),
        mesh=mesh,
        in_specs=(P("band", "grid", None), P()),
        out_specs=P("band", "grid", None),
        check_vma=False,
    )
```

time: 86.6 us -> 73.8 us (0.85)
  Pallas kernels: 81.9 us -> 71.6 us
  local copies, waits for them, and re-layouts: 4.38 us -> 2.06 us
    pallas_call x1, Pallas kernels: 81.9 us -> 71.6 us  [local(): pl.pallas_call(functools.partial(kernel, groups), out_shape=jax.ShapeDtyp...]
    unnamed x9 -> x1, local copies, waits for them, and re-layouts: 4.38 us -> 2.06 us
where the time goes in v1:
time: 73.8 us; the launch traced here: 73.6 us
  Pallas kernels  71.6 us (97%)
  local copies, waits for them, and re-layouts  2.06 us (3%)
    pallas_call x1, Pallas kernels, local(): pl.pallas_call(functools.partial(kernel, groups), out_shape=jax.ShapeDtyp...  71.6 us
    unnamed x1, local copies, waits for them, and re-layouts  2.06 us

profile of v1, /device:TPU:0, one launch (start us, length us, event | category | flops | bytes accessed | tf_op | source)
XLA Modules:
  0.0 73.6 jit_solution(10257978254081063399)
XLA Ops:
  0.0 71.6 %shard_map.46 = f32[3,16,4096]{2,1,0:T(8,128)} custom-call(s32[24,24]{1,0:T(8,128)} %mask_hbm.1, f32[3,16,4096]{2,1,0:T(8,128)} %mine_ref.1, bf16[128,128]{1,0:T(8,128)(2,1)} %constant.4.clone.left_hbm, bf16[256,256]{1,0:T(8,128)(2,1)} %constant.5.clone.right_hbm), custom_call_target="tpu_custom_call" | custom-call | tf_op jit(solution)/shard_map/pallas_call | solution.py:498
  71.6 2.1 %copy.6 = f32[3,16,4096]{2,1,0:T(8,128)} copy(f32[3,16,4096]{2,1,0:T(8,128)} %shard_map.46) | data formatting | bytes 1572864

commit v2 on v1

--- a/solution.py
+++ b/solution.py
@@ -14,21 +14,44 @@
 BOX_LENGTH = 16.0
 SKEW = 4
 
-CHUNKS = 2
+HALVES = 2
+SMALL = ((0, 0, 1), (0, 1, 1), (0, 2, 2), (0, 4, 4), (1, 0, 8))
+HALF = ((0, 0, 8), (1, 0, 8))
+
+
+TAIL = ((0, 0, 8), (1, 0, 4), (1, 4, 2), (1, 6, 2))
+
+
+def pieces(cuts):
+    return [(k, row, 1, column, parts) for k, cut in enumerate(cuts) for row, column, parts in cut]
+
+
+AHEAD = BACK = pieces((SMALL, HALF, HALF, TAIL))
+JOINED_BEFORE = (0, (2, 0, 1, 0, 8))
+
+
+def in_order_of_arrival(cuts):
+    hop, sent, free, events = 0.3, 0.0, 0.0, []
+    for m, piece in enumerate(cuts):
+        size = piece[4] / 16
+        sent += size
+        free = max(free, sent + hop) + size
+        events += [(sent + hop, 0, m), (free + hop, 1, m)]
+    return [(what, m) for _, what, m in sorted(events)]
 
 PEER = 0
 CROSS = PEER + 3
-RELAY = CROSS + 3 * CHUNKS
-DOWN = RELAY + 3 * CHUNKS
-SIDE = DOWN + 4 * CHUNKS
-SIDE_BACK = SIDE + 4 * CHUNKS
-UP_BACK = SIDE_BACK + 4 * CHUNKS
-JOINT = UP_BACK + 4 * CHUNKS
+RELAY = CROSS + 3 * HALVES
+DOWN = RELAY + 3 * HALVES
+SIDE = DOWN + len(AHEAD)
+SIDE_BACK = SIDE + len(AHEAD)
+UP_BACK = SIDE_BACK + len(BACK)
+JOINT = UP_BACK + len(BACK)
 COMB = JOINT + 3
 FROM_PEER = COMB + 2
-FROM_CHIP = FROM_PEER + 3 * CHUNKS
-FAR = FROM_CHIP + 3 * CHUNKS
-COPIES = FAR + CHUNKS
+FROM_CHIP = FROM_PEER + 3
+FAR = FROM_CHIP + 3
+COPIES = FAR + 1
 
 
 def transform_tables(n):
@@ -107,14 +130,15 @@
             work[pl.ds(y * stride + start, planes), :] = along_z[u * planes:(u + 1) * planes]
 
 
-def along_y(n, planes, work, left_ref, quarter):
+def along_y(n, planes, works, left_ref, quarter):
     stride = n + SKEW
     left = left_ref[...]
-    for u in range(planes // 2):
-        here = [pl.ds(quarter * planes + 2 * u + j, n, stride=stride) for j in range(2)]
-        done = left_product(left, jnp.concatenate([work[h, :] for h in here], axis=1))
-        work[here[0], :] = done[:, :2 * n]
-        work[here[1], :] = done[:, 2 * n:]
+    for work in works:
+        for u in range(planes // 2):
+            here = [pl.ds(quarter * planes + 2 * u + j, n, stride=stride) for j in range(2)]
+            done = left_product(left, jnp.concatenate([work[h, :] for h in here], axis=1))
+            work[here[0], :] = done[:, :2 * n]
+            work[here[1], :] = done[:, 2 * n:]
 
 
 def along_x(n, work, coulomb, left_ref):
@@ -163,11 +187,10 @@
 
 
 def kernel(groups, mask_hbm, mine_ref, left_hbm, right_hbm, out_ref,
-           phi, pot, coulomb, work, side, up, comb, joint, from_peer, from_chip,
+           phi, pot, coulomb, work, side, up, comb, joint, from_peer, from_chip, result,
            left_ref, right_ref, mask_ref, load_sem, send_sem, recv_sem):
     orbs, planes, cells = mine_ref.shape
     n = phi.shape[1]
-    depth = planes // CHUNKS
     band, grid = lax.axis_index("band"), lax.axis_index("grid")
     last = grid // orbs
     odd_band = lax.rem(band, 2)
@@ -179,14 +202,24 @@
     odd_shares = shares & (odd_band == 1)
 
     def order(device):
-        first = device - device // orbs
-        second = 1 - (device + 2) // orbs
+        first, second = 2 * (device // 2), 1 - device // 2
         return first, second, orbs - first - second
 
     def rows(quarter):
         return pl.ds(pl.multiple_of(quarter * planes, planes), planes)
 
-    def part(quarter, c):
+    depth, width = planes // 2, cells // 8
+
+    def inner(piece):
+        _, row, halves, column, parts = piece
+        return pl.ds(row * depth, halves * depth), pl.ds(column * width, parts * width)
+
+    def part(quarter, piece):
+        _, row, halves, column, parts = piece
+        first = pl.multiple_of(quarter * planes + row * depth, depth)
+        return pl.ds(first, halves * depth), pl.ds(column * width, parts * width)
+
+    def half(quarter, c):
         return pl.ds(pl.multiple_of(quarter * planes + c * depth, depth), depth)
 
     def copy(source, target, number, device, sent=None):
@@ -215,55 +248,61 @@
 
     quarters = (grid, peer, across, far)
 
-    def pass_on(k, c):
-        piece = phi.at[lax.rem(grid, orbs), part(quarters[k], c)]
-
-        @pl.when(shares)
-        def _():
-            copy(piece, phi.at[4, part(quarters[k], c)], DOWN + k * CHUNKS + c, (below, grid)).start()
-
-        @pl.when(odd_shares)
-        def _():
-            copy(piece, phi.at[3, part(quarters[k], c)], SIDE + k * CHUNKS + c, (beside, grid)).start()
+    def pass_on(k, only=None):
+        for m, piece in enumerate(AHEAD):
+            if piece[0] != k or only not in (None, piece[1]):
+                continue
+            here = part(quarters[k], piece)
+            source = phi.at[lax.rem(grid, orbs), *here]
+
+            @pl.when(shares)
+            def _():
+                copy(source, phi.at[4, *here], DOWN + m, (below, grid)).start()
+
+            @pl.when(odd_shares)
+            def _():
+                copy(source, phi.at[3, *here], SIDE + m, (beside, grid)).start()
 
     def side_relay(m):
-        k, c = divmod(m, CHUNKS)
-        piece = phi.at[4, part(quarters[k], c)]
+        here = part(quarters[AHEAD[m][0]], AHEAD[m])
 
         @pl.when(even_shares)
         def _():
-            arrived(piece, DOWN + m)
-            copy(piece, phi.at[3, part(quarters[k], c)], SIDE + m, (beside, grid)).start()
-
-    for c in range(CHUNKS):
-        pass_on(0, c)
+            arrived(phi.at[4, *here], DOWN + m)
+            copy(phi.at[4, *here], phi.at[3, *here], SIDE + m, (beside, grid)).start()
+
+    def side_relays(k):
+        return [m for m, piece in enumerate(AHEAD) if piece[0] == k]
+
+    first_turn, second_turn = grid != 1, grid == 1
+    pl.when(first_turn)(lambda: pass_on(0))
     for k, i in enumerate(order(across)):
-        for c in range(CHUNKS):
-            piece = phi.at[i, part(grid, c)]
-            copy(piece, piece, CROSS + k * CHUNKS + c, (band, across)).start()
+        for c in range(HALVES):
+            piece = phi.at[i, half(grid, c)]
+            copy(piece, piece, CROSS + k * HALVES + c, (band, across)).start()
     for k, i in enumerate(order(peer)):
         piece = phi.at[i, rows(grid)]
         copy(piece, piece, PEER + k, (band, peer)).start()
 
     mine, theirs = order(grid), order(peer)
-    arrived(phi.at[mine[0], rows(peer)], PEER)
-    for c in range(CHUNKS):
-        pass_on(1, c)
+    for k in range(orbs):
+        arrived(phi.at[mine[k], rows(peer)], PEER + k)
+    pl.when(first_turn)(lambda: pass_on(1))
     fill_coulomb(n, coulomb)
     for load in loads[orbs:]:
         load.wait()
 
     def relay(k, c):
-        piece = phi.at[mine[k], part(across, c)]
-        arrived(piece, CROSS + k * CHUNKS + c)
-        copy(piece, piece, RELAY + k * CHUNKS + c, (band, peer)).start()
-
-    wanted = 1 - grid // 2
+        piece = phi.at[mine[k], half(across, c)]
+        arrived(piece, CROSS + k * HALVES + c)
+        copy(piece, piece, RELAY + k * HALVES + c, (band, peer)).start()
+
+    wanted = lax.rem(grid, 2)
 
     def far_on(c):
         @pl.when(shares)
         def _():
-            arrived(phi.at[grid, part(far, c)], RELAY + wanted * CHUNKS + c)
+            arrived(phi.at[grid, half(far, c)], RELAY + wanted * HALVES + c)
 
         pass_on(3, c)
 
@@ -271,7 +310,7 @@
         within = lax.rem(i + 1 - near, orbs)
         return last * within + (1 - last) * (4 - near)
 
-    def forward(p, quarter):
+    def density(p, quarter):
         pairs = []
         for lane_half in range(2):
             number = 2 * p + lane_half
@@ -281,101 +320,162 @@
             weight = mask_ref[band * orbs + i, column].astype(jnp.float32)
             pairs.append((i, partner(i, near), weight))
         densities(n, planes, phi, work.at[p], right_ref, quarter, pairs)
-        along_y(n, planes, work.at[p], left_ref, quarter)
-
-    def forward_rest(quarter):
-        def body(p, carry):
-            forward(p, quarter)
-            return carry
-
-        lax.fori_loop(1, 3, body, 0)
 
     def await_down(k):
         @pl.when(odd_shares)
         def _():
-            for c in range(CHUNKS):
-                arrived(phi.at[4, part(quarters[k], c)], DOWN + k * CHUNKS + c)
+            for m in side_relays(k):
+                arrived(phi.at[4, *part(quarters[k], AHEAD[m])], DOWN + m)
 
     def await_side(k):
         @pl.when(shares)
         def _():
-            for c in range(CHUNKS):
-                arrived(phi.at[3, part(quarters[k], c)], SIDE + k * CHUNKS + c)
-
-    zero = lax.rem(grid, 1)
-    for c in range(CHUNKS):
-        relay(0, c)
-        pass_on(2, c)
-        side_relay(c)
-    await_down(0)
-    forward(zero, quarters[0])
-    for c in range(CHUNKS):
-        relay(1, c)
-        side_relay(CHUNKS + c)
-        far_on(c)
-    await_down(1)
-    for k in range(1, orbs):
-        arrived(phi.at[mine[k], rows(peer)], PEER + k)
-    forward(zero, quarters[1])
-    for c in range(CHUNKS):
-        side_relay(2 * CHUNKS + c)
-        relay(2, c)
-    await_down(2)
-    forward(zero, quarters[2])
-    for c in range(CHUNKS - 1):
-        side_relay(3 * CHUNKS + c)
-    for k in range(2):
-        await_side(k)
-        forward_rest(quarters[k])
-    side_relay(4 * CHUNKS - 1)
-    for k in range(orbs):
-        @pl.when((last == 1) | (k != wanted))
-        def _():
-            for c in range(CHUNKS):
-                arrived(phi.at[theirs[k], part(far, c)], RELAY + k * CHUNKS + c)
-    await_down(3)
-    forward(zero, quarters[3])
-
-    def solve(p, carry):
-        @pl.when(p == 1)
-        def _():
-            for k in (2, 3):
-                await_side(k)
-                forward_rest(quarters[k])
-
-        along_x(n, work.at[p], coulomb, left_ref)
+            for m in side_relays(k):
+                arrived(phi.at[3, *part(quarters[k], AHEAD[m])], SIDE + m)
+
+    def choose(index, values):
+        chosen = values[0]
+        for position, value in enumerate(values[1:], 1):
+            chosen = jnp.where(index == position, value, chosen)
+        return chosen
+
+    def relayed(k, rows_only=None):
+        for m in side_relays(k):
+            if rows_only in (None, AHEAD[m][1]):
+                side_relay(m)
+
+    def all_relayed():
+        for k in range(orbs):
+            @pl.when((last == 1) | (k != wanted))
+            def _():
+                for c in range(HALVES):
+                    arrived(phi.at[theirs[k], half(far, c)], RELAY + k * HALVES + c)
+
+    def early_0():
+        relayed(0, 0)
+        relay(0, 0)
+        pass_on(2, 0)
+        relayed(0, 1)
+        far_on(0)
+        await_down(0)
+
+    def early_1():
+        relayed(1, 0)
+        relay(0, 1)
+        pass_on(2, 1)
+        relayed(1, 1)
+        far_on(1)
+        await_down(1)
+
+    def early_2():
+        relayed(2, 0)
+        await_side(0)
+
+    def early_3():
+        relayed(2, 1)
+        relay(1, 0)
+        await_side(1)
+
+    def early_4():
+        relayed(3)
+        relay(1, 1)
+        relay(2, 0)
+        relay(2, 1)
+        await_down(2)
+
+    def early_6():
+        all_relayed()
+        await_down(3)
+
+    def late_0():
+        for k in range(2):
+            for c in range(HALVES):
+                relay(k, c)
+        for k in range(3):
+            pass_on(k)
+        relayed(0, 0)
+        relay(2, 0)
+        far_on(0)
+        far_on(1)
+        relayed(0, 1)
+        relay(2, 1)
+        await_down(0)
+
+    def late_1():
+        relayed(1)
+        await_down(1)
+
+    def late_3():
+        relayed(2)
+        await_side(1)
+
+    def late_5():
+        relayed(3, 0)
+        await_side(2)
+
+    def late_6():
+        relayed(3, 1)
+        all_relayed()
+        await_down(3)
+
+    first_work, other_works, along = range(3)
+    steps = ((first_work, 0), (first_work, 1), (other_works, 0), (other_works, 1), (first_work, 2),
+             (other_works, 2), (first_work, 3), (along, 0), (other_works, 3), (along, 1), (along, 2))
+    early = {0: early_0, 1: early_1, 2: early_2, 3: early_3, 4: early_4, 5: lambda: await_side(2), 6: early_6}
+    late = {0: late_0, 1: late_1, 2: lambda: await_side(0), 3: late_3, 4: lambda: await_down(2),
+            5: late_5, 6: late_6}
+
+    def step(index, carry):
+        for turn, actions in ((first_turn, early), (second_turn, late)):
+            for position, action in actions.items():
+                pl.when(turn & (index == position))(action)
+        pl.when(index == 8)(lambda: await_side(3))
+        kind = choose(index, [which for which, _ in steps])
+        number = choose(index, [k for _, k in steps])
+        quarter = choose(number, quarters)
+
+        @pl.when(kind == first_work)
+        def _():
+            density(0, quarter)
+            along_y(n, planes, [work.at[0]], left_ref, quarter)
+
+        @pl.when(kind == other_works)
+        def _():
+            density(1, quarter)
+            density(2, quarter)
+            along_y(n, planes, [work.at[1], work.at[2]], left_ref, quarter)
+
+        @pl.when(kind == along)
+        def _():
+            along_x(n, work.at[number], coulomb, left_ref)
+
         return carry
 
-    lax.fori_loop(0, 3, solve, 0)
+    lax.fori_loop(0, len(steps), step, 0)
 
     back = (across, far, peer, grid)
     partners = [[partner(i, near) for i in range(3)] for near in range(2)]
 
     def up_send(m):
-        k, c = divmod(m, CHUNKS)
-        copy(pot.at[4, part(back[k], c)], up.at[part(back[k], c)], UP_BACK + m, (above, grid)).start()
+        here = part(back[BACK[m][0]], BACK[m])
+        copy(pot.at[4, *here], up.at[*here], UP_BACK + m, (above, grid)).start()
 
     def elsewhere(i):
         return grid // 2 != i // 2
 
-    for k in range(4):
-        def inverse(p, carry):
-            along_y(n, planes, work.at[p], left_ref, back[k])
-            return carry
-
-        lax.fori_loop(0, 3, inverse, 0)
-        exchange_terms(n, planes, phi, pot, work, right_ref, back[k], last, partners)
-
+    def send_back(k):
         @pl.when(shares)
         def _():
-            for c in range(CHUNKS):
-                here = part(back[k], c)
-                copy(pot.at[3, here], side.at[here], SIDE_BACK + k * CHUNKS + c, (beside, grid)).start()
+            for m, piece in enumerate(BACK):
+                if piece[0] == k:
+                    here = part(back[k], piece)
+                    copy(pot.at[3, *here], side.at[*here], SIDE_BACK + m, (beside, grid)).start()
 
         @pl.when(odd_shares)
         def _():
-            for c in range(CHUNKS):
-                up_send(k * CHUNKS + c)
+            for m, piece in enumerate(BACK):
+                if piece[0] == k:
+                    up_send(m)
 
         if k == 1:
             for i in range(orbs):
@@ -392,101 +492,107 @@
             for i in range(orbs):
                 @pl.when(elsewhere(i) | (peer == i))
                 def _():
-                    for c in range(CHUNKS):
-                        copy(pot.at[i, part(peer, c)], from_peer.at[i, pl.ds(c * depth, depth)],
-                             FROM_PEER + i * CHUNKS + c, (band, peer)).start()
-
-    for i in range(orbs):
-        @pl.when(elsewhere(i))
-        def _():
-            arrived(joint.at[i], JOINT + i)
-            pot[i, rows(across), :] += joint[i]
-            for c in range(CHUNKS):
-                copy(pot.at[i, part(across, c)], from_chip.at[i, pl.ds(c * depth, depth)],
-                     FROM_CHIP + i * CHUNKS + c, (band, across)).start()
+                    copy(pot.at[i, rows(peer)], from_peer.at[i], FROM_PEER + i, (band, peer)).start()
+
+    def back_step(index, carry):
+        quarter = choose(index, back)
+
+        along_y(n, planes, [work.at[p] for p in range(3)], left_ref, quarter)
+        exchange_terms(n, planes, phi, pot, work, right_ref, quarter, last, partners)
+        for k in range(4):
+            pl.when(index == k)(functools.partial(send_back, k))
+        return carry
+
+    lax.fori_loop(0, 4, back_step, 0)
 
     def join(m):
-        k, c = divmod(m, CHUNKS)
+        here = part(back[BACK[m][0]], BACK[m])
 
         @pl.when(even_shares)
         def _():
-            arrived(side.at[part(back[k], c)], SIDE_BACK + m)
-            pot[4, part(back[k], c), :] += side[part(back[k], c), :]
+            arrived(side.at[*here], SIDE_BACK + m)
+            pot[4, *here] += side[*here]
             up_send(m)
 
     def collect(m):
-        k, c = divmod(m, CHUNKS)
-        here = part(back[k], c)
-        inner = pl.ds(c * depth, depth)
+        k = BACK[m][0]
+        here, within = part(back[k], BACK[m]), inner(BACK[m])
 
         @pl.when(shares)
         def _():
-            if k < 2 and c == 0:
+            if k < 2 and BACK[m - 1][0] != k:
                 arrived(comb.at[k], COMB + k)
-            arrived(up.at[here], UP_BACK + m)
+            arrived(up.at[*here], UP_BACK + m)
             if k < 2:
-                pot[grid, here, :] += up[here, :] + comb[k, inner, :]
+                pot[grid, *here] += up[*here] + comb[k, *within]
             else:
-                pot[grid, here, :] += up[here, :]
+                pot[grid, *here] += up[*here]
 
         @pl.when(odd_shares)
         def _():
-            arrived(side.at[here], SIDE_BACK + m)
-            pot[grid, here, :] += side[here, :]
+            arrived(side.at[*here], SIDE_BACK + m)
+            pot[grid, *here] += side[*here]
 
         @pl.when(shares)
         def _():
-            source = pot.at[grid, here]
-            number = grid * CHUNKS + c
+            source = pot.at[grid, *here]
             if k == 0:
-                copy(source, from_chip.at[grid, inner], FROM_CHIP + number, (band, across)).start()
+                copy(source, from_chip.at[grid, *within], FROM_CHIP + grid, (band, across)).start()
             elif k == 1:
-                copy(source, from_chip.at[grid, inner], FROM_CHIP + number, (band, far), FAR + c).start()
+                copy(source, from_chip.at[grid, *within], FROM_CHIP + grid, (band, far), FAR).start()
             elif k == 2:
-                copy(source, from_peer.at[grid, inner], FROM_PEER + number, (band, peer)).start()
-
-    join(0)
-    join(1)
-    for m in range(4 * CHUNKS):
-        collect(m)
-        if m + 2 < 4 * CHUNKS:
-            join(m + 2)
-
-    for i in range(orbs):
-        for c in range(CHUNKS):
-            inner = pl.ds(c * depth, depth)
-            arrived(from_peer.at[i, inner], FROM_PEER + i * CHUNKS + c)
-            arrived(from_chip.at[i, inner], FROM_CHIP + i * CHUNKS + c)
-        out_ref[i] = pot[i, rows(grid), :] + from_peer[i] + from_chip[i]
-
-    whole, chunk = comb.at[0], comb.at[0, pl.ds(0, depth)]
+                copy(source, from_peer.at[grid, *within], FROM_PEER + grid, (band, peer)).start()
+
+    def finish(i, k):
+        arrived(from_peer.at[i], FROM_PEER + i)
+        arrived(from_chip.at[i], FROM_CHIP + i)
+        result[i] = pot[i, rows(grid), :] + from_peer[i] + from_chip[i]
+        pltpu.make_async_copy(result.at[i], out_ref.at[i], load_sem.at[k]).start()
+
+    def joined():
+        for i in range(orbs):
+            @pl.when(elsewhere(i))
+            def _():
+                arrived(joint.at[i], JOINT + i)
+                pot[i, rows(across), :] += joint[i]
+                copy(pot.at[i, rows(across)], from_chip.at[i], FROM_CHIP + i, (band, across)).start()
+
+    for what, m in in_order_of_arrival(BACK):
+        if (what, BACK[m]) == JOINED_BEFORE:
+            joined()
+        (collect if what else join)(m)
+    soon = choose(grid, (2, 2, 0, 0))
+    own = choose(grid, (0, 1, 2, 2))
+    for k, i in enumerate((soon, orbs - soon - own, own)):
+        finish(i, k)
+
+    whole, halved = comb.at[0], comb.at[0, pl.ds(0, planes // HALVES)]
     for number in range(PEER, PEER + 3):
         gone(whole, number)
     for number in range(CROSS, DOWN):
-        gone(chunk, number)
+        gone(halved, number)
 
     @pl.when(shares)
     def _():
-        for number in (*range(DOWN, JOINT), *range(FAR, FAR + CHUNKS)):
-            gone(chunk, number)
-        for c in range(CHUNKS):
-            gone(chunk, FROM_CHIP + grid * CHUNKS + c)
-            gone(chunk, FROM_PEER + grid * CHUNKS + c)
+        for first, cuts in ((DOWN, AHEAD), (SIDE, AHEAD), (SIDE_BACK, BACK), (UP_BACK, BACK)):
+            for m, piece in enumerate(cuts):
+                gone(comb.at[0, *inner(piece)], first + m)
+        for number in (FROM_CHIP + grid, FROM_PEER + grid, FAR):
+            gone(whole, number)
 
     @pl.when(peer_shares)
     def _():
-        gone(whole, COMB)
-        gone(whole, COMB + 1)
-        for c in range(CHUNKS):
-            gone(chunk, FROM_PEER + peer * CHUNKS + c)
+        for number in (COMB, COMB + 1, FROM_PEER + peer):
+            gone(whole, number)
 
     for i in range(orbs):
         @pl.when(elsewhere(i))
         def _():
-            gone(whole, JOINT + i)
-            for c in range(CHUNKS):
-                gone(chunk, FROM_PEER + i * CHUNKS + c)
-                gone(chunk, FROM_CHIP + i * CHUNKS + c)
+            for number in (JOINT + i, FROM_PEER + i, FROM_CHIP + i):
+                gone(whole, number)
+
+    for k in range(orbs):
+        pltpu.make_async_copy(result.at[k], out_ref.at[k], load_sem.at[k]).wait()
 
 
 def local(groups, orbitals, pair_mask):
@@ -499,7 +605,7 @@
         functools.partial(kernel, groups),
         out_shape=jax.ShapeDtypeStruct(orbitals.shape, jnp.float32),
         in_specs=[in_hbm] * 4,
-        out_specs=pl.BlockSpec(memory_space=pltpu.VMEM),
+        out_specs=in_hbm,
         scratch_shapes=[
             pltpu.VMEM((orbs + 2, *cube), jnp.float32),
             pltpu.VMEM((orbs + 2, *cube), jnp.float32),
@@ -508,6 +614,7 @@
             pltpu.VMEM(cube, jnp.float32),
             pltpu.VMEM(cube, jnp.float32),
             pltpu.VMEM((2, *piece), jnp.float32),
+            pltpu.VMEM((orbs, *piece), jnp.float32),
             pltpu.VMEM((orbs, *piece), jnp.float32),
             pltpu.VMEM((orbs, *piece), jnp.float32),
             pltpu.VMEM((orbs, *piece), jnp.float32),

time: 73.8 us -> 71.3 us (0.966)
  the two profiles are of different devices: /device:TPU:0 before, /device:TPU:1 now
where the time goes in v2:
time: 71.3 us; the launch traced here: 71.1 us
  Pallas kernels  69 us (97%)
  local copies, waits for them, and re-layouts  2.06 us (3%)
    pallas_call x1, Pallas kernels, local(): pl.pallas_call(functools.partial(kernel, groups), out_shape=jax.ShapeDtyp...  69 us
    unnamed x1, local copies, waits for them, and re-layouts  2.06 us

profile of v2, /device:TPU:1, one launch (start us, length us, event | category | flops | bytes accessed | tf_op | source)
XLA Modules:
  0.0 71.1 jit_solution(11120248279555755510)
XLA Ops:
  0.0 69.0 %shard_map.46 = f32[3,16,4096]{2,1,0:T(8,128)} custom-call(s32[24,24]{1,0:T(8,128)} %mask_hbm.1, f32[3,16,4096]{2,1,0:T(8,128)} %mine_ref.1, bf16[128,128]{1,0:T(8,128)(2,1)} %constant.4.clone.left_hbm, bf16[256,256]{1,0:T(8,128)(2,1)} %constant.5.clone.right_hbm), custom_call_target="tpu_custom_call" | custom-call | tf_op jit(solution)/shard_map/pallas_call | solution.py:604
  69.0 2.1 %copy.6 = f32[3,16,4096]{2,1,0:T(8,128)} copy(f32[3,16,4096]{2,1,0:T(8,128)} %shard_map.46) | data formatting | bytes 1572864

commit v3 on v2

--- a/solution.py
+++ b/solution.py
@@ -31,12 +31,12 @@
 
 
 def in_order_of_arrival(cuts):
-    hop, sent, free, events = 0.3, 0.0, 0.0, []
+    hop, delay, sent, free, events = 0.3, 1.0, 0.0, 0.0, []
     for m, piece in enumerate(cuts):
         size = piece[4] / 16
         sent += size
         free = max(free, sent + hop) + size
-        events += [(sent + hop, 0, m), (free + hop, 1, m)]
+        events += [(sent + hop, 0, m), (free + hop + delay, 1, m)]
     return [(what, m) for _, what, m in sorted(events)]
 
 PEER = 0

time: 71.3 us -> 68.6 us (0.962)
  Pallas kernels: 69 us -> 66.4 us
    pallas_call x1, Pallas kernels: 69 us -> 66.4 us  [local(): pl.pallas_call(functools.partial(kernel, groups), out_shape=jax.ShapeDtyp...]
where the time goes in v3:
time: 68.6 us; the launch traced here: 68.4 us
  Pallas kernels  66.4 us (97%)
  local copies, waits for them, and re-layouts  2.06 us (3%)
    pallas_call x1, Pallas kernels, local(): pl.pallas_call(functools.partial(kernel, groups), out_shape=jax.ShapeDtyp...  66.4 us
    unnamed x1, local copies, waits for them, and re-layouts  2.06 us

profile of v3, /device:TPU:1, one launch (start us, length us, event | category | flops | bytes accessed | tf_op | source)
XLA Modules:
  0.0 68.4 jit_solution(17375658539234459973)
XLA Ops:
  0.0 66.4 %shard_map.46 = f32[3,16,4096]{2,1,0:T(8,128)} custom-call(s32[24,24]{1,0:T(8,128)} %mask_hbm.1, f32[3,16,4096]{2,1,0:T(8,128)} %mine_ref.1, bf16[128,128]{1,0:T(8,128)(2,1)} %constant.4.clone.left_hbm, bf16[256,256]{1,0:T(8,128)(2,1)} %constant.5.clone.right_hbm), custom_call_target="tpu_custom_call" | custom-call | tf_op jit(solution)/shard_map/pallas_call | solution.py:604
  66.4 2.1 %copy.6 = f32[3,16,4096]{2,1,0:T(8,128)} copy(f32[3,16,4096]{2,1,0:T(8,128)} %shard_map.46) | data formatting | bytes 1572864

commit v4 on v3

--- a/solution.py
+++ b/solution.py
@@ -15,18 +15,14 @@
 SKEW = 4
 
 HALVES = 2
-SMALL = ((0, 0, 1), (0, 1, 1), (0, 2, 2), (0, 4, 4), (1, 0, 8))
 HALF = ((0, 0, 8), (1, 0, 8))
-
-
-TAIL = ((0, 0, 8), (1, 0, 4), (1, 4, 2), (1, 6, 2))
 
 
 def pieces(cuts):
     return [(k, row, 1, column, parts) for k, cut in enumerate(cuts) for row, column, parts in cut]
 
 
-AHEAD = BACK = pieces((SMALL, HALF, HALF, TAIL))
+AHEAD = BACK = pieces((HALF, HALF, HALF, HALF))
 JOINED_BEFORE = (0, (2, 0, 1, 0, 8))
 
 

time: 68.6 us -> 67.2 us (0.980)
  Pallas kernels: 66.4 us -> 65 us
    pallas_call x1, Pallas kernels: 66.4 us -> 65 us  [local(): pl.pallas_call(functools.partial(kernel, groups), out_shape=jax.ShapeDtyp...]
where the time goes in v4:
time: 67.2 us; the launch traced here: 67 us
  Pallas kernels  65 us (97%)
  local copies, waits for them, and re-layouts  2.06 us (3%)
    pallas_call x1, Pallas kernels, local(): pl.pallas_call(functools.partial(kernel, groups), out_shape=jax.ShapeDtyp...  65 us
    unnamed x1, local copies, waits for them, and re-layouts  2.06 us

profile of v4, /device:TPU:1, one launch (start us, length us, event | category | flops | bytes accessed | tf_op | source)
XLA Modules:
  0.0 67.0 jit_solution(15839681258726757263)
XLA Ops:
  0.0 65.0 %shard_map.46 = f32[3,16,4096]{2,1,0:T(8,128)} custom-call(s32[24,24]{1,0:T(8,128)} %mask_hbm.1, f32[3,16,4096]{2,1,0:T(8,128)} %mine_ref.1, bf16[128,128]{1,0:T(8,128)(2,1)} %constant.4.clone.left_hbm, bf16[256,256]{1,0:T(8,128)(2,1)} %constant.5.clone.right_hbm), custom_call_target="tpu_custom_call" | custom-call | tf_op jit(solution)/shard_map/pallas_call | solution.py:600
  65.0 2.1 %copy.6 = f32[3,16,4096]{2,1,0:T(8,128)} copy(f32[3,16,4096]{2,1,0:T(8,128)} %shard_map.46) | data formatting | bytes 1572864
